TPU v7x, 32 devices: a whole 2x2x4 slice. The times are simulated.
32 devices in a mesh: cuts: 8 (over z, y), batch: 4 (over x, core).
Axes of the slice: x: 2, y: 2, z: 4, core: 2. Of those that a mesh axis runs over, the one named last changes fastest.
Arguments:
- blocks: bfloat16 [256, 64, 128], P(('cuts', 'batch')), may hold values from -6 to 6
- environments: bfloat16 [256, 64, 128], P(('cuts', 'batch')), may hold values from -0.5 to 0.5
- layers: bfloat16 [8, 64, 128], replicated, may hold values from -0.5 to 0.5
- selectors: bfloat16 [256, 8, 128], P(('cuts', 'batch')), may hold values from -6 to 6
- classes: int32 [32, 8], P(('cuts', 'batch')), may hold values from 1 to 8
- routing: int32 [32, 8], P(('cuts', 'batch')), may hold values from 0 to 7, each once within a row
- left_edges: bfloat16 [64, 128], replicated, may hold values from -0.5 to 0.5
- right_edges: bfloat16 [64, 128], replicated, may hold values from -0.5 to 0.5
- owner_map: int32 [4096], replicated, may hold values from 0 to 4095, each once
Outputs:
- amplitudes: float32 [2, 4096], P(None, ('cuts', 'batch'))
Inputs may be any that keep to these rules, and one draw needn't show every extreme that they name: `routing`: each holder's row is a permutation of 0 to 7. `owner_map`: A permutation of the bitstrings.
All inputs are finite; a program needn't handle non-finite values.
Results may differ from a plain program's by a relative error of at most 0.009.
Values may be sent and summed in bfloat16 or wider, within the bound.
A program may use at most 64 MiB of HBM per device.

v0:
```python
import jax
import jax.numpy as jnp
from jax import lax
from jax.sharding import PartitionSpec as P


def block_form(matrix):
    half_count = matrix.shape[-1] // 2
    real_block = matrix[..., :half_count]
    imag_block = matrix[..., half_count:]
    upper_rows = jnp.concatenate([real_block, imag_block], axis=-1)
    lower_rows = jnp.concatenate([-imag_block, real_block], axis=-1)
    return jnp.concatenate([upper_rows, lower_rows], axis=-2)


def apply_phase(product, factors):
    half_count = product.shape[-1] // 2
    prod_real = product[..., :half_count]
    prod_imag = product[..., half_count:]
    fac_real = factors[..., :half_count].astype(jnp.float32)[:, None, :]
    fac_imag = factors[..., half_count:].astype(jnp.float32)[:, None, :]
    out_real = prod_real * fac_real - prod_imag * fac_imag
    out_imag = prod_real * fac_imag + prod_imag * fac_real
    return jnp.concatenate([out_real, out_imag], axis=-1)


def advance(blocks_now, factors, levels, tables):
    slot_count = blocks_now.shape[0]
    block_rows = min(32, slot_count)
    ranking = jnp.argsort(-levels, stable=True)
    blocks_now = blocks_now[ranking]
    factors = factors[ranking]
    levels = levels[ranking]
    for layer_index in range(tables.shape[0]):
        active = jnp.sum((levels > layer_index).astype(jnp.int32))
        rounds = (active + block_rows - 1) // block_rows
        layer_factors = factors[:, layer_index, :]

        def apply(round_index, current, layer_index=layer_index, layer_factors=layer_factors):
            offset = round_index * block_rows
            portion = lax.dynamic_slice_in_dim(current, offset, block_rows, 0)
            portion_levels = lax.dynamic_slice_in_dim(levels, offset, block_rows, 0)
            portion_factors = lax.dynamic_slice_in_dim(layer_factors, offset, block_rows, 0)
            product = jnp.einsum(
                "sij,jk->sik", portion, tables[layer_index], preferred_element_type=jnp.float32
            )
            updated = apply_phase(product, portion_factors).astype(jnp.bfloat16)
            portion = jnp.where((portion_levels > layer_index)[:, None, None], updated, portion)
            return lax.dynamic_update_slice_in_dim(current, portion, offset, 0)

        blocks_now = lax.fori_loop(0, rounds, apply, blocks_now)
    return (blocks_now, ranking)


def contract(worked, partners):
    slot_count, bond_width, doubled = worked.shape
    parted = worked.reshape(slot_count, bond_width, 2, bond_width)
    products = jnp.einsum("sipj,sjk->pik", parted, partners, preferred_element_type=jnp.float32)
    real_part = products[0, :, :bond_width] - products[1, :, bond_width:]
    imag_part = products[0, :, bond_width:] + products[1, :, :bond_width]
    return (real_part, imag_part)


def amplitude_table(real_part, imag_part, left_edges, right_edges, owner_map):
    highest = lax.Precision.HIGHEST
    half_count = left_edges.shape[1] // 2
    left_real = left_edges[:, :half_count].astype(jnp.float32)
    left_imag = left_edges[:, half_count:].astype(jnp.float32)
    right_real = right_edges[:, :half_count].astype(jnp.float32)
    right_imag = right_edges[:, half_count:].astype(jnp.float32)
    wave_real = jnp.dot(real_part, right_real, precision=highest) - jnp.dot(
        imag_part, right_imag, precision=highest
    )
    wave_imag = jnp.dot(real_part, right_imag, precision=highest) + jnp.dot(
        imag_part, right_real, precision=highest
    )
    amp_real = jnp.dot(left_real.T, wave_real, precision=highest) - jnp.dot(
        left_imag.T, wave_imag, precision=highest
    )
    amp_imag = jnp.dot(left_real.T, wave_imag, precision=highest) + jnp.dot(
        left_imag.T, wave_real, precision=highest
    )
    flattened = jnp.stack([amp_real.reshape(-1), amp_imag.reshape(-1)])
    return flattened[:, owner_map]


def on_device(
    blocks, environments, layers, selectors, classes, routing, left_edges, right_edges, owner_map
):
    slot_count, bond_width, doubled = blocks.shape
    cut_count = lax.axis_size("cuts")
    member = slot_count // cut_count
    tables = block_form(layers)
    levels = classes[0]
    sending = routing[0]
    worked, ranking = advance(blocks, selectors, levels, tables)
    inverse = jnp.argsort(ranking)
    outgoing = worked[inverse[sending]].reshape(cut_count, member, bond_width, doubled)
    worked = lax.all_to_all(outgoing, "cuts", split_axis=0, concat_axis=0, tiled=True).reshape(
        slot_count, bond_width, doubled
    )
    real_part, imag_part = contract(worked, environments)
    holder_count = cut_count * lax.axis_size("batch")
    normalizer = (slot_count * holder_count) ** (-0.5)
    real_part, imag_part = lax.psum((real_part, imag_part), ("cuts", "batch"))
    amp_table = (
        amplitude_table(real_part, imag_part, left_edges, right_edges, owner_map) * normalizer
    )
    per_holder = amp_table.shape[1] // holder_count
    holder = lax.axis_index("cuts") * lax.axis_size("batch") + lax.axis_index("batch")
    return lax.dynamic_slice_in_dim(amp_table, holder * per_holder, per_holder, 1)


def solution(mesh):
    placed = (
        P(("cuts", "batch"), None, None),
        P(("cuts", "batch"), None, None),
        P(),
        P(("cuts", "batch"), None, None),
        P(("cuts", "batch"), None),
        P(("cuts", "batch"), None),
        P(),
        P(),
        P(),
    )
    return jax.shard_map(
        on_device, mesh=mesh, in_specs=placed, out_specs=P(None, ("cuts", "batch")), check_vma=False
    )
```

profile of v0, /device:TPU:0, one launch (start us, length us, event | category | flops | bytes accessed | tf_op | source)
XLA Modules:
  0.0 92.2 jit_solution(10878997560112806243)
XLA Ops:
  0.0 0.7 bitcast_negate_fusion
  0.7 1.0 %sort.34 = (s32[8]{0:T(128)}, s32[8]{0:T(128)S(1)}) sort(s32[8]{0:T(128)S(1)} %bitcast_negate_fusion, s32[8]{0:T(128)S(1)} %iota.8), dimensions={0}, to_apply=%region_0.0 | sort | flops 24 | bytes 128 | tf_op jit(solution)/shard_map/jit(argsort)/sort | solution.py:30
  1.7 1.3 %gather_fusion.1 = s32[8]{0:T(128)S(1)} fusion(s32[8]{0:T(128)} %bitcast.127, s32[1024]{0:T(1024)S(1)} %pad_clamp_fusion.2), kind=kCustom, calls=%fused_computation.1 | custom fusion | bytes 96 | tf_op jit(solution)/shard_map/gather | solution.py:33
  3.0 0.8 fusion.51
  8.8 1.3 %gather_fusion.2 = bf16[8,8,128]{2,1,0:T(8,128)(2,1)S(1)} fusion(bf16[8,8,128]{2,1,0:T(8,128)(2,1)} %param.28, s32[1024]{0:T(1024)S(1)} %pad_clamp_fusion.2), kind=kCustom, calls=%fused_computation.2 | custom fusion | bytes 32800 | tf_op jit(solution)/shard_map/gather | solution.py:32
  10.1 1.1 %slice_negate_fusion = (bf16[8,64,64]{2,1,0:T(8,128)(2,1)S(1)}, bf16[8,64,64]{2,1,0:T(8,128)(2,1)S(1)}) fusion(bf16[8,64,128]{2,1,0:T(8,128)(2,1)} %param.27), kind=kLoop, calls=%fused_computation.88 | loop fusion | flops 32768 | bytes 262144 | tf_op jit(solution)/shard_map/neg | solution.py:12
  11.2 0.6 gather_fusion
  11.8 1.0 %maximum_maximum_fusion = bf16[8,128,128]{2,1,0:T(8,128)(2,1)S(1)} fusion(bf16[8,64,64]{2,1,0:T(8,128)(2,1)S(1)} %get-tuple-element.420, bf16[8,64,64]{2,1,0:T(8,128)(2,1)S(1)} %get-tuple-element.419, bf16[8,64,128]{2,1,0:T(8,128)(2,1)} %param.27), kind=kLoop, calls=%fused_computation.85 | loop fusion | flops 786432 | bytes 524288 | tf_op jit(solution)/shard_map/concatenate | solution.py:13
  12.8 0.6 while.80
  12.9 0.2 fusion.97
  13.5 0.6 while.81
  13.5 0.2 fusion.100
  14.1 0.6 while.82
  14.1 0.2 fusion.103
  14.4 0.2 subtract_convert_fusion.18
  15.0 1.0 %sort.35 = (s32[8]{0:T(128)}, s32[8]{0:T(128)S(1)}) sort(s32[8]{0:T(128)S(1)} %get-tuple-element.271, s32[8]{0:T(128)S(1)} %iota.9), dimensions={0}, to_apply=%region_25.26 | sort | flops 24 | bytes 128 | tf_op jit(solution)/shard_map/jit(argsort)/sort | solution.py:97
  16.0 0.6 gather_fusion.3
  16.6 1.2 %gather_fusion.4 = bf16[8,64,128]{2,1,0:T(8,128)(2,1)} fusion(bf16[8,64,128]{2,1,0:T(8,128)(2,1)S(1)} %get-tuple-element.279, s32[1024]{0:T(1024)S(1)} %pad_clamp_fusion), kind=kCustom, calls=%fused_computation.4 | custom fusion | bytes 262176 | tf_op jit(solution)/shard_map/gather | solution.py:98
  17.8 10.2 %all-to-all-start = ((bf16[8,1,64,128]{3,2,1,0:T(8,128)(2,1)}), bf16[8,1,64,128]{3,2,1,0:T(8,128)(2,1)S(1)}, u32[]{:S(2)}, u32[]{:S(2)}) async-start(bf16[8,1,64,128]{3,2,1,0:T(8,128)(2,1)} %bitcast.21), calls=%async_computation | async-start | bytes 262144 | tf_op jit(solution)/shard_map/all_to_all | solution.py:99
  28.1 7.3 %all-to-all-done = bf16[8,1,64,128]{3,2,1,0:T(8,128)(2,1)S(1)} async-done(((bf16[8,1,64,128]{3,2,1,0:T(8,128)(2,1)}), bf16[8,1,64,128]{3,2,1,0:T(8,128)(2,1)S(1)}, u32[]{:S(2)}, u32[]{:S(2)}) %all-to-all-start) | async-done | bytes 131104 | tf_op jit(solution)/shard_map/all_to_all | solution.py:99
  35.5 0.2 convolution_bitcast_fusion
  35.9 38.0 %all-reduce = (f32[64,64]{1,0:T(8,128)S(1)}, f32[64,64]{1,0:T(8,128)S(1)}) all-reduce(f32[64,64]{1,0:T(8,128)S(1)} %get-tuple-element.422, f32[64,64]{1,0:T(8,128)S(1)} %get-tuple-element.421), channel_id=1, replica_groups=mesh['cuts'=8,'batch'=4] {'cuts','batch'}, use_global_device_ids=true, to_apply=%region_26.27 | all-reduce | flops 8192 | bytes 65536 | tf_op jit(solution)/shard_map/psum | solution.py:105
  74.1 0.2 fusion.38
  74.3 0.2 convolution_subtract_fusion.1
  74.7 0.2 fusion.36
  74.9 0.2 fusion.34
  75.1 0.2 fusion.25
  75.5 0.2 fusion.24
  76.0 0.6 copy.26
  76.6 14.1 %gather_fusion.5 = f32[4096,2]{1,0:T(8,128)} fusion(f32[2,4096]{0,1:T(8,128)S(1)} %copy.26, s32[4096]{0:T(1024)S(1)} %fusion.31), kind=kCustom, calls=%fused_computation.5 | custom fusion | bytes 81920 | tf_op jit(solution)/shard_map/gather | solution.py:84
  90.7 0.8 fusion.28
  91.6 0.6 copy.27
  (51 shorter events, 2.0 us)
Async XLA Ops:
  0.0 11.2 %copy-start = (bf16[8,64,128]{2,1,0:T(8,128)(2,1)S(1)}, bf16[8,64,128]{2,1,0:T(8,128)(2,1)}, u32[]{:S(2)}) copy-start(bf16[8,64,128]{2,1,0:T(8,128)(2,1)} %param.25) | copy-start | bytes 393220
  14.9 1.1 %copy-start.5 = (s32[1,8]{1,0:T(1,128)S(1)}, s32[1,8]{1,0:T(1,128)}, u32[]{:S(2)}) copy-start(s32[1,8]{1,0:T(1,128)} %param.30) | copy-start | bytes 100
  14.9 13.1 %copy-start.3 = (s32[4096]{0:T(1024)S(1)}, s32[4096]{0:T(1024)}, u32[]{:S(2)}) copy-start(s32[4096]{0:T(1024)} %param.33) | copy-start | bytes 49156
  14.9 20.6 %copy-start.4 = (bf16[8,64,128]{2,1,0:T(8,128)(2,1)S(1)}, bf16[8,64,128]{2,1,0:T(8,128)(2,1)}, u32[]{:S(2)}) copy-start(bf16[8,64,128]{2,1,0:T(8,128)(2,1)} %param.26) | copy-start | bytes 393220
  15.0 59.0 %copy-start.1 = (bf16[64,128]{1,0:T(8,128)(2,1)S(1)}, bf16[64,128]{1,0:T(8,128)(2,1)}, u32[]{:S(2)}) copy-start(bf16[64,128]{1,0:T(8,128)(2,1)} %param.32) | copy-start | bytes 49156
  15.0 59.7 %copy-start.2 = (bf16[64,128]{1,0:T(8,128)(2,1)S(1)}, bf16[64,128]{1,0:T(8,128)(2,1)}, u32[]{:S(2)}) copy-start(bf16[64,128]{1,0:T(8,128)(2,1)} %param.31) | copy-start | bytes 49156
  17.8 17.6 %all-to-all-start = ((bf16[8,1,64,128]{3,2,1,0:T(8,128)(2,1)}), bf16[8,1,64,128]{3,2,1,0:T(8,128)(2,1)S(1)}, u32[]{:S(2)}, u32[]{:S(2)}) async-start(bf16[8,1,64,128]{3,2,1,0:T(8,128)(2,1)} %bitcast.21), calls=%async_computation | async-start | bytes 262144 | tf_op jit(solution)/shard_map/all_to_all | solution.py:99
where the time goes:
time: 92.8 us; the launch traced here: 92.2 us
  blocking collectives  38 us (41%)
  local copies, waits for them, and re-layouts  20.9 us (23%)
  starting transfers between devices  10.2 us (11%)
  other arithmetic  7.64 us (8%)
  waiting for transfers between devices  7.32 us (8%)
  between operations  5.54 us (6%)
  matrix products  2.34 us (3%)
    psum x1, blocking collectives, on_device(): real_part, imag_part = lax.psum((real_part, imag_part), ('cuts', 'batch'))  38 us
    gather x1, local copies, waits for them, and re-layouts, amplitude_table(): return flattened[:, owner_map]  14.1 us
    all_to_all x1, starting transfers between devices, on_device(): lax.all_to_all(outgoing, 'cuts', split_axis=0, concat_axis=0, tiled=True)  10.2 us
    all_to_all x1, waiting for transfers between devices, on_device(): lax.all_to_all(outgoing, 'cuts', split_axis=0, concat_axis=0, tiled=True)  7.32 us
  transfers between devices with their start and end apart: 1, of which 1 were waited for; matrix products, arithmetic and copies ran while one was open for 0% of the time, Pallas kernels for 0%

commit v1 on v0

--- a/solution.py
+++ b/solution.py
@@ -2,6 +2,38 @@
 import jax.numpy as jnp
 from jax import lax
 from jax.sharding import PartitionSpec as P
+from jax.lax import axis_index, axis_size, ppermute
+
+
+def sums_all_read(arr, dimension_no, local_array):
+    aux = arr.shape
+    right_arr = arr.reshape(
+        *aux[:dimension_no], local_array, aux[dimension_no] // local_array, *aux[dimension_no + 1 :]
+    )
+    return jnp.moveaxis(right_arr, dimension_no, 0)
+
+
+def table_shape(obj, axis_no):
+    obj = jnp.moveaxis(obj, 0, axis_no)
+    d_next = obj.shape
+    return obj.reshape(
+        *d_next[:axis_no], d_next[axis_no] * d_next[axis_no + 1], *d_next[axis_no + 2 :]
+    )
+
+
+def lead_the_slabs(u_in, bus_axis, mine, chunk):
+    k_now = axis_index(bus_axis)
+    block_next = axis_size(bus_axis)
+    local_out, w_next = (block_next, k_now)
+    local_part = sums_all_read(u_in, mine, local_out)
+    views = [local_part[w_next]]
+    for h in range(1, local_out):
+        tmp = local_part[(w_next + h) % local_out]
+        even = ppermute(tmp, bus_axis, [(j, (j + h) % local_out) for j in range(local_out)])
+        views.append(even)
+    taken_in = jnp.stack(views, 0)
+    local_part = taken_in[(w_next - jnp.arange(local_out)) % local_out]
+    return table_shape(local_part, chunk)
 
 
 def block_form(matrix):
@@ -96,9 +128,7 @@
     worked, ranking = advance(blocks, selectors, levels, tables)
     inverse = jnp.argsort(ranking)
     outgoing = worked[inverse[sending]].reshape(cut_count, member, bond_width, doubled)
-    worked = lax.all_to_all(outgoing, "cuts", split_axis=0, concat_axis=0, tiled=True).reshape(
-        slot_count, bond_width, doubled
-    )
+    worked = lead_the_slabs(outgoing, "cuts", 0, 0).reshape(slot_count, bond_width, doubled)
     real_part, imag_part = contract(worked, environments)
     holder_count = cut_count * lax.axis_size("batch")
     normalizer = (slot_count * holder_count) ** (-0.5)

time: 92.8 us -> 104 us (1.12)
  waiting for transfers between devices: 7.32 us -> 15.9 us
  starting transfers between devices: 10.2 us -> 13.9 us
  other arithmetic: 7.64 us -> 6.6 us
    ppermute x0 -> x7, waiting for transfers between devices: none -> 15.9 us  [lead_the_slabs(): ppermute(tmp, bus_axis, [(j, (j + h) % local_out) for j in range(local_ou...]
    ppermute x0 -> x7, starting transfers between devices: none -> 13.9 us  [lead_the_slabs(): ppermute(tmp, bus_axis, [(j, (j + h) % local_out) for j in range(local_ou...]
    all_to_all x1 -> x0, starting transfers between devices: 10.2 us -> none  [on_device(): lax.all_to_all(outgoing, 'cuts', split_axis=0, concat_axis=0, tiled=True)]
    all_to_all x1 -> x0, waiting for transfers between devices: 7.32 us -> none  [on_device(): lax.all_to_all(outgoing, 'cuts', split_axis=0, concat_axis=0, tiled=True)]
  transfers between devices with their start and end apart: 1 -> 7, of which waited for: 1 -> 3; matrix products, arithmetic and copies ran while one was open for 0% -> 0% of each run, Pallas kernels for 0% -> 0%
where the time goes in v1:
time: 104 us; the launch traced here: 103 us
  blocking collectives  37.3 us (36%)
  local copies, waits for them, and re-layouts  21 us (20%)
  waiting for transfers between devices  15.9 us (15%)
  starting transfers between devices  13.9 us (13%)
  other arithmetic  6.6 us (6%)
  between operations  5.71 us (5%)
  matrix products  2.34 us (2%)
    psum x1, blocking collectives, on_device(): real_part, imag_part = lax.psum((real_part, imag_part), ('cuts', 'batch'))  37.3 us
    ppermute x7, waiting for transfers between devices, lead_the_slabs(): ppermute(tmp, bus_axis, [(j, (j + h) % local_out) for j in range(local_ou...  15.9 us
    gather x1, local copies, waits for them, and re-layouts, amplitude_table(): return flattened[:, owner_map]  14.1 us
    ppermute x7, starting transfers between devices, lead_the_slabs(): ppermute(tmp, bus_axis, [(j, (j + h) % local_out) for j in range(local_ou...  13.9 us
  transfers between devices with their start and end apart: 7, of which 3 were waited for; matrix products, arithmetic and copies ran while one was open for 0% of the time, Pallas kernels for 0%

profile of v1, /device:TPU:0, one launch (start us, length us, event | category | flops | bytes accessed | tf_op | source)
XLA Modules:
  0.0 103.0 jit_solution(4827590776523225360)
XLA Ops:
  0.0 0.7 fusion.53
  0.7 0.7 bitcast_negate_fusion
  1.4 1.0 %sort.34 = (s32[8]{0:T(128)}, s32[8]{0:T(128)S(1)}) sort(s32[8]{0:T(128)S(1)} %bitcast_negate_fusion, s32[8]{0:T(128)S(1)} %iota.12), dimensions={0}, to_apply=%region_0.0 | sort | flops 24 | bytes 128 | tf_op jit(solution)/shard_map/jit(argsort)/sort | solution.py:62
  2.4 1.0 %sort.35 = (s32[8]{0:T(128)}, s32[8]{0:T(128)S(1)}) sort(s32[8]{0:T(128)S(1)} %get-tuple-element.271, s32[8]{0:T(128)S(1)} %iota.13), dimensions={0}, to_apply=%region_25.26 | sort | flops 24 | bytes 128 | tf_op jit(solution)/shard_map/jit(argsort)/sort | solution.py:129
  3.4 0.6 gather_fusion.3
  4.1 1.3 %gather_fusion.1 = s32[8]{0:T(128)S(1)} fusion(s32[8]{0:T(128)} %bitcast.165, s32[1024]{0:T(1024)S(1)} %get-tuple-element.439), kind=kCustom, calls=%fused_computation.1 | custom fusion | bytes 96 | tf_op jit(solution)/shard_map/gather | solution.py:65
  5.4 0.8 fusion.51
  11.4 1.3 %gather_fusion.2 = bf16[8,8,128]{2,1,0:T(8,128)(2,1)S(1)} fusion(bf16[8,8,128]{2,1,0:T(8,128)(2,1)} %param.28, s32[1024]{0:T(1024)S(1)} %get-tuple-element.439), kind=kCustom, calls=%fused_computation.2 | custom fusion | bytes 32800 | tf_op jit(solution)/shard_map/gather | solution.py:64
  12.8 0.6 gather_fusion
  13.6 0.6 while.80
  14.2 0.6 while.81
  14.8 0.6 while.82
  15.6 0.6 gather_fusion.4
  16.2 9.0 %collective-permute-start.6 = (bf16[1,1,64,128]{3,2,1,0:T(8,128)(2,1)S(1)}, bf16[1,1,64,128]{3,2,1,0:T(8,128)(2,1)S(1)}, u32[]{:S(2)}, u32[]{:S(2)}) collective-permute-start(bf16[1,1,64,128]{3,2,1,0:T(8,128)(2,1)S(1)} %get-tuple-element.419), channel_id=1, source_target_pairs={{0,28},{4,0},{8,4},{12,8},{16,12},{20,16},{24,20},{28,24},{1,29},{... | collective-permute-start | bytes 49160 | tf_op jit(solution)/shard_map/ppermute | solution.py:32
  25.2 3.4 %collective-permute-start.3 = (bf16[1,1,64,128]{3,2,1,0:T(8,128)(2,1)S(1)}, bf16[1,1,64,128]{3,2,1,0:T(8,128)(2,1)S(1)}, u32[]{:S(2)}, u32[]{:S(2)}) collective-permute-start(bf16[1,1,64,128]{3,2,1,0:T(8,128)(2,1)S(1)} %get-tuple-element.422), channel_id=1, source_target_pairs={{0,16},{4,20},{8,24},{12,28},{16,0},{20,4},{24,8},{28,12},{1,17},{... | collective-permute-start | bytes 49160 | tf_op jit(solution)/shard_map/ppermute | solution.py:32
  28.6 1.5 %collective-permute-start = (bf16[1,1,64,128]{3,2,1,0:T(8,128)(2,1)S(1)}, bf16[1,1,64,128]{3,2,1,0:T(8,128)(2,1)S(1)}, u32[]{:S(2)}, u32[]{:S(2)}) collective-permute-start(bf16[1,1,64,128]{3,2,1,0:T(8,128)(2,1)S(1)} %get-tuple-element.425), channel_id=1, source_target_pairs={{0,4},{4,8},{8,12},{12,16},{16,20},{20,24},{24,28},{28,0},{1,5},{5... | collective-permute-start | bytes 49160 | tf_op jit(solution)/shard_map/ppermute | solution.py:32
  30.2 4.8 %collective-permute-done = bf16[1,1,64,128]{3,2,1,0:T(8,128)(2,1)S(1)} collective-permute-done((bf16[1,1,64,128]{3,2,1,0:T(8,128)(2,1)S(1)}, bf16[1,1,64,128]{3,2,1,0:T(8,128)(2,1)S(1)}, u32[]{:S(2)}, u32[]{:S(2)}) %collective-permute-start) | collective-permute-done | bytes 16416 | tf_op jit(solution)/shard_map/ppermute | solution.py:32
  35.1 5.5 %collective-permute-done.1 = bf16[1,1,64,128]{3,2,1,0:T(8,128)(2,1)S(1)} collective-permute-done((bf16[1,1,64,128]{3,2,1,0:T(8,128)(2,1)S(1)}, bf16[1,1,64,128]{3,2,1,0:T(8,128)(2,1)S(1)}, u32[]{:S(2)}, u32[]{:S(2)}) %collective-permute-start.1) | collective-permute-done | bytes 16416 | tf_op jit(solution)/shard_map/ppermute | solution.py:32
  40.6 5.5 %collective-permute-done.2 = bf16[1,1,64,128]{3,2,1,0:T(8,128)(2,1)S(1)} collective-permute-done((bf16[1,1,64,128]{3,2,1,0:T(8,128)(2,1)S(1)}, bf16[1,1,64,128]{3,2,1,0:T(8,128)(2,1)S(1)}, u32[]{:S(2)}, u32[]{:S(2)}) %collective-permute-start.2) | collective-permute-done | bytes 16416 | tf_op jit(solution)/shard_map/ppermute | solution.py:32
  46.2 0.6 gather_fusion.5
  47.0 0.2 convolution_bitcast_fusion
  47.3 37.3 %all-reduce = (f32[64,64]{1,0:T(8,128)S(1)}, f32[64,64]{1,0:T(8,128)S(1)}) all-reduce(f32[64,64]{1,0:T(8,128)S(1)} %get-tuple-element.429, f32[64,64]{1,0:T(8,128)S(1)} %get-tuple-element.428), channel_id=1, replica_groups=mesh['cuts'=8,'batch'=4] {'cuts','batch'}, use_global_device_ids=true, to_apply=%region_26.27 | all-reduce | flops 8192 | bytes 65536 | tf_op jit(solution)/shard_map/psum | solution.py:135
  84.7 0.2 fusion.38
  85.2 0.2 convolution_subtract_fusion.1
  85.4 0.2 fusion.36
  85.6 0.2 fusion.34
  85.8 0.2 fusion.25
  86.1 0.2 fusion.24
  86.7 0.7 copy.26
  87.4 14.1 %gather_fusion.6 = f32[4096,2]{1,0:T(8,128)} fusion(f32[2,4096]{0,1:T(8,128)S(1)} %copy.26, s32[4096]{0:T(1024)S(1)} %fusion.31), kind=kCustom, calls=%fused_computation.6 | custom fusion | bytes 81920 | tf_op jit(solution)/shard_map/gather | solution.py:116
  101.5 0.8 fusion.28
  102.3 0.6 copy.27
  (78 shorter events, 3.0 us)
Async XLA Ops:
  0.0 12.8 %copy-start = (bf16[8,64,128]{2,1,0:T(8,128)(2,1)S(1)}, bf16[8,64,128]{2,1,0:T(8,128)(2,1)}, u32[]{:S(2)}) copy-start(bf16[8,64,128]{2,1,0:T(8,128)(2,1)} %param.25) | copy-start | bytes 393220
  0.0 13.4 %copy-start.1 = (bf16[8,64,128]{2,1,0:T(8,128)(2,1)S(1)}, bf16[8,64,128]{2,1,0:T(8,128)(2,1)}, u32[]{:S(2)}) copy-start(bf16[8,64,128]{2,1,0:T(8,128)(2,1)} %param.27) | copy-start | bytes 393220
  15.5 14.7 %copy-start.4 = (s32[4096]{0:T(1024)S(1)}, s32[4096]{0:T(1024)}, u32[]{:S(2)}) copy-start(s32[4096]{0:T(1024)} %param.33) | copy-start | bytes 49156
  15.5 31.4 %copy-start.5 = (bf16[8,64,128]{2,1,0:T(8,128)(2,1)S(1)}, bf16[8,64,128]{2,1,0:T(8,128)(2,1)}, u32[]{:S(2)}) copy-start(bf16[8,64,128]{2,1,0:T(8,128)(2,1)} %param.26) | copy-start | bytes 393220
  15.6 69.1 %copy-start.2 = (bf16[64,128]{1,0:T(8,128)(2,1)S(1)}, bf16[64,128]{1,0:T(8,128)(2,1)}, u32[]{:S(2)}) copy-start(bf16[64,128]{1,0:T(8,128)(2,1)} %param.32) | copy-start | bytes 49156
  15.6 69.8 %copy-start.3 = (bf16[64,128]{1,0:T(8,128)(2,1)S(1)}, bf16[64,128]{1,0:T(8,128)(2,1)}, u32[]{:S(2)}) copy-start(bf16[64,128]{1,0:T(8,128)(2,1)} %param.31) | copy-start | bytes 49156
  16.2 30.0 %collective-permute-start.6 = (bf16[1,1,64,128]{3,2,1,0:T(8,128)(2,1)S(1)}, bf16[1,1,64,128]{3,2,1,0:T(8,128)(2,1)S(1)}, u32[]{:S(2)}, u32[]{:S(2)}) collective-permute-start(bf16[1,1,64,128]{3,2,1,0:T(8,128)(2,1)S(1)} %get-tuple-element.419), channel_id=1, source_target_pairs={{0,28},{4,0},{8,4},{12,8},{16,12},{20,16},{24,20},{28,24},{1,29},{... | collective-permute-start | bytes 49160 | tf_op jit(solution)/shard_map/ppermute | solution.py:32
  25.2 21.0 %collective-permute-start.5 = (bf16[1,1,64,128]{3,2,1,0:T(8,128)(2,1)S(1)}, bf16[1,1,64,128]{3,2,1,0:T(8,128)(2,1)S(1)}, u32[]{:S(2)}, u32[]{:S(2)}) collective-permute-start(bf16[1,1,64,128]{3,2,1,0:T(8,128)(2,1)S(1)} %get-tuple-element.420), channel_id=1, source_target_pairs={{0,24},{4,28},{8,0},{12,4},{16,8},{20,12},{24,16},{28,20},{1,25},{... | collective-permute-start | bytes 49160 | tf_op jit(solution)/shard_map/ppermute | solution.py:32
  25.2 21.0 %collective-permute-start.4 = (bf16[1,1,64,128]{3,2,1,0:T(8,128)(2,1)S(1)}, bf16[1,1,64,128]{3,2,1,0:T(8,128)(2,1)S(1)}, u32[]{:S(2)}, u32[]{:S(2)}) collective-permute-start(bf16[1,1,64,128]{3,2,1,0:T(8,128)(2,1)S(1)} %get-tuple-element.421), channel_id=1, source_target_pairs={{0,20},{4,24},{8,28},{12,0},{16,4},{20,8},{24,12},{28,16},{1,21},{... | collective-permute-start | bytes 49160 | tf_op jit(solution)/shard_map/ppermute | solution.py:32
  25.2 21.0 %collective-permute-start.3 = (bf16[1,1,64,128]{3,2,1,0:T(8,128)(2,1)S(1)}, bf16[1,1,64,128]{3,2,1,0:T(8,128)(2,1)S(1)}, u32[]{:S(2)}, u32[]{:S(2)}) collective-permute-start(bf16[1,1,64,128]{3,2,1,0:T(8,128)(2,1)S(1)} %get-tuple-element.422), channel_id=1, source_target_pairs={{0,16},{4,20},{8,24},{12,28},{16,0},{20,4},{24,8},{28,12},{1,17},{... | collective-permute-start | bytes 49160 | tf_op jit(solution)/shard_map/ppermute | solution.py:32
  28.6 6.4 %collective-permute-start = (bf16[1,1,64,128]{3,2,1,0:T(8,128)(2,1)S(1)}, bf16[1,1,64,128]{3,2,1,0:T(8,128)(2,1)S(1)}, u32[]{:S(2)}, u32[]{:S(2)}) collective-permute-start(bf16[1,1,64,128]{3,2,1,0:T(8,128)(2,1)S(1)} %get-tuple-element.425), channel_id=1, source_target_pairs={{0,4},{4,8},{8,12},{12,16},{16,20},{20,24},{24,28},{28,0},{1,5},{5... | collective-permute-start | bytes 49160 | tf_op jit(solution)/shard_map/ppermute | solution.py:32
  35.1 5.5 %collective-permute-start.1 = (bf16[1,1,64,128]{3,2,1,0:T(8,128)(2,1)S(1)}, bf16[1,1,64,128]{3,2,1,0:T(8,128)(2,1)S(1)}, u32[]{:S(2)}, u32[]{:S(2)}) collective-permute-start(bf16[1,1,64,128]{3,2,1,0:T(8,128)(2,1)S(1)} %get-tuple-element.424), channel_id=1, source_target_pairs={{0,8},{4,12},{8,16},{12,20},{16,24},{20,28},{24,0},{28,4},{1,9},{5... | collective-permute-start | bytes 49160 | tf_op jit(solution)/shard_map/ppermute | solution.py:32
  40.6 5.5 %collective-permute-start.2 = (bf16[1,1,64,128]{3,2,1,0:T(8,128)(2,1)S(1)}, bf16[1,1,64,128]{3,2,1,0:T(8,128)(2,1)S(1)}, u32[]{:S(2)}, u32[]{:S(2)}) collective-permute-start(bf16[1,1,64,128]{3,2,1,0:T(8,128)(2,1)S(1)} %get-tuple-element.423), channel_id=1, source_target_pairs={{0,12},{4,16},{8,20},{12,24},{16,28},{20,0},{24,4},{28,8},{1,13},{... | collective-permute-start | bytes 49160 | tf_op jit(solution)/shard_map/ppermute | solution.py:32
